TPU v7x, 32 devices: a whole 2x2x4 slice. The times are simulated.
32 devices in a mesh: dp: 8 (over z, y), mp: 4 (over x, core).
Axes of the slice: x: 2, y: 2, z: 4, core: 2. Of those that a mesh axis runs over, the one named last changes fastest.
Arguments:
- tokens: bfloat16 [8, 1024, 1280], P('dp', 'mp'), may hold values from -6 to 6
- sizes: float32 [8, 1024], P('dp'), may hold values from 1 to 8
- ln1_gain: float32 [1280], replicated, may hold values from 0.25 to 1.75
- qkv_weight: bfloat16 [3, 1280, 1280], P(None, 'dp', 'mp'), may hold values from -0.15625 to 0.15625
- proj_weight: bfloat16 [1280, 1280], P('mp', 'dp'), may hold values from -0.15625 to 0.15625
- ln2_gain: float32 [1280], replicated, may hold values from 0.25 to 1.75
- fc1_weight: bfloat16 [1280, 5120], P('dp', 'mp'), may hold values from -0.15625 to 0.15625
- fc1_bias: float32 [5120], P('mp'), may hold values from -3 to 3
- fc2_weight: bfloat16 [5120, 1280], P('mp', 'dp'), may hold values from -0.078125 to 0.078125
- pair_source: int32 [8, 16], P('dp'), may hold values from 0 to 1022, as said below
- pair_target: int32 [8, 16], P('dp'), may hold values from 1 to 1023, as said below
- kept_order: int32 [8, 1008], P('dp'), may hold values from 0 to 1023, as said below
Outputs:
- merged_out: bfloat16 [8, 1008, 1280], P('dp', 'mp')
Inputs may be any that keep to these rules, and one draw needn't show every extreme that they name: `pair_source`: in each image the 16 entries are distinct even token indices. `pair_target`: odd token indices; several sources may join the same target. `kept_order`: in each image every token index that is not in pair_source appears exactly once.
All inputs are finite; a program needn't handle non-finite values.
Results may differ from a plain program's by a relative error of at most 0.017.
Values may be sent and summed in bfloat16 or wider, within the bound.
A program may use at most 64 MiB of HBM per device.

v0:
```python
import math
import jax
import jax.numpy as jnp
from jax import lax
from jax.sharding import PartitionSpec as P

D = 1280
HEADS = 16


def layer_norm(values, gain):
    center = values - jnp.mean(values, axis=-1, keepdims=True)
    spread = jnp.mean(center * center, axis=-1, keepdims=True)
    return center * lax.rsqrt(spread + 1e-06) * gain


def merge_rows(total, order_rows, source_ids, target_ids):
    kept_rows = jnp.take_along_axis(total, order_rows[:, :, None], axis=1)
    source_rows = jnp.take_along_axis(total, source_ids[:, :, None], axis=1)
    joins = (order_rows[:, :, None] == target_ids[:, None, :]).astype(jnp.float32)
    return kept_rows + jnp.einsum(
        "icr,ird->icd", joins, source_rows, precision=lax.Precision.HIGHEST
    )


def shards(
    tokens,
    sizes,
    ln1_gain,
    qkv_weight,
    proj_weight,
    ln2_gain,
    fc1_weight,
    fc1_bias,
    fc2_weight,
    pair_source,
    pair_target,
    kept_order,
):
    images, own_tokens, width = tokens.shape
    length = sizes.shape[1]
    kept_total = kept_order.shape[1]
    devices_mp = lax.axis_size("mp")
    own_start = lax.axis_index("mp") * own_tokens
    head_size = D // HEADS
    base = tokens.astype(jnp.float32)
    normed = layer_norm(base, ln1_gain).astype(jnp.bfloat16)
    whole = lax.all_gather(normed, "mp", axis=1, tiled=True)
    local_width = qkv_weight.shape[2]
    columns = whole
    projected = jnp.einsum(
        "ind,cdf->cinf",
        columns,
        lax.all_gather(qkv_weight, "dp", axis=1, tiled=True),
        preferred_element_type=jnp.float32,
    ).astype(jnp.bfloat16)
    local_heads = local_width // head_size
    shaped = projected.reshape(3, images, length, local_heads, head_size)
    queries = shaped[0]
    keys_all = shaped[1]
    values_all = shaped[2]
    size_bias = jnp.log(sizes)[:, None, None, :]
    block = min(512, length)
    outputs = []
    for begin in range(0, length, block):
        scores = (
            jnp.einsum(
                "iqhe,ikhe->ihqk",
                queries[:, begin : begin + block],
                keys_all,
                preferred_element_type=jnp.float32,
            )
            / math.sqrt(head_size)
            + size_bias
        )
        weights = jax.nn.softmax(scores, axis=-1).astype(jnp.bfloat16)
        attended_block = jnp.einsum(
            "ihqk,ikhe->iqhe", weights, values_all, preferred_element_type=jnp.float32
        )
        outputs.append(attended_block.astype(jnp.bfloat16).reshape(images, block, local_width))
    attended = jnp.concatenate(outputs, axis=1)
    branch = jnp.einsum(
        "ind,de->ine",
        attended,
        lax.all_gather(proj_weight, "dp", axis=1, tiled=True),
        preferred_element_type=jnp.float32,
    )
    weighted = sizes[:, :, None] * branch
    own_sizes = lax.dynamic_slice_in_dim(sizes, own_start, own_tokens, 1)
    own_weighted = own_sizes[:, :, None] * base
    local_total = lax.dynamic_update_slice_in_dim(
        weighted,
        lax.dynamic_slice_in_dim(weighted, own_start, own_tokens, 1) + own_weighted,
        own_start,
        1,
    )
    merged_count = kept_total // devices_mp
    own_order = lax.dynamic_slice_in_dim(
        kept_order, lax.axis_index("mp") * merged_count, merged_count, 1
    )
    scattered = lax.psum_scatter(
        jnp.transpose(
            merge_rows(local_total, kept_order, pair_source, pair_target), (1, 0, 2)
        ).astype(jnp.bfloat16),
        "mp",
        scatter_dimension=0,
        tiled=True,
    ).astype(jnp.float32)
    numerator = jnp.transpose(scattered, (1, 0, 2))
    merged_size = merge_rows(sizes[:, :, None], own_order, pair_source, pair_target)
    merged = numerator / merged_size
    normed_two = layer_norm(merged, ln2_gain).astype(jnp.bfloat16)
    gathered = lax.all_gather(normed_two, "mp", axis=1, tiled=True)
    columns = gathered
    hidden_sum = jnp.einsum(
        "imd,df->imf",
        columns,
        lax.all_gather(fc1_weight, "dp", axis=0, tiled=True),
        preferred_element_type=jnp.float32,
    )
    hidden = jax.nn.gelu(hidden_sum + fc1_bias).astype(jnp.bfloat16)
    partial_out = jnp.einsum(
        "imf,fd->imd",
        hidden,
        lax.all_gather(fc2_weight, "dp", axis=1, tiled=True),
        preferred_element_type=jnp.float32,
    )
    mlp_part = lax.psum_scatter(
        partial_out.astype(jnp.bfloat16), "mp", scatter_dimension=1, tiled=True
    ).astype(jnp.float32)
    return (merged + mlp_part).astype(jnp.bfloat16)


def solution(mesh):
    return jax.shard_map(
        shards,
        mesh=mesh,
        in_specs=(
            P("dp", "mp", None),
            P("dp", None),
            P(),
            P(None, "dp", "mp"),
            P("mp", "dp"),
            P(),
            P("dp", "mp"),
            P("mp"),
            P("mp", "dp"),
            P("dp", None),
            P("dp", None),
            P("dp", None),
        ),
        out_specs=P("dp", "mp", None),
        check_vma=False,
    )
```

profile of v0, /device:TPU:1, one launch (start us, length us, event | category | flops | bytes accessed | tf_op | source)
XLA Modules:
  0.0 317.7 jit_solution(4380768634615341311)
XLA Ops:
  6.6 1.3 convert_reduce_fusion
  7.9 1.4 fusion.30
  9.3 2.2 fusion.32
  11.6 0.7 all-gather.8.cloned.1.call-update
  12.4 0.7 all-gather.12.cloned.1.call-update
  13.8 28.3 %all_gather.20 = bf16[320,1280]{0,1:T(8,128)(2,1)S(1)} all-gather(bf16[320,160]{0,1:T(8,128)(2,1)S(1)} %copy-done.2), channel_id=1, replica_groups=mesh['dp'=8,'mp'=4] {'dp'}, dimensions={1}, use_global_device_ids=true | all-gather | bytes 921600 | tf_op jit(solution)/shard_map/all_gather | solution.py:85
  42.8 1.4 gather_fusion.2
  44.4 53.4 %all-gather.8.cloned.1.call-done = bf16[3,1280,320]{2,1,0:T(8,128)(2,1)} async-done(((bf16[3,160,320]{2,1,0:T(8,128)(2,1)}), bf16[3,1280,320]{2,1,0:T(8,128)(2,1)}) %all-gather.8.cloned.1.call-update) | async-done | bytes 2457616 | tf_op jit(solution)/shard_map/all_gather | solution.py:54
  97.8 5.4 %convert_bitcast_fusion = bf16[3,1,1024,320]{2,3,0,1:T(8,128)(2,1)S(1)} fusion(bf16[3,1280,320]{2,1,0:T(8,128)(2,1)} %all-gather.8.cloned.1.call-done, bf16[1,1024,1280]{2,1,0:T(8,128)(2,1)} %all-gather.6.cloned.1.call-done), kind=kOutput, calls=%fused_computation.38 | convolution fusion | flops 2517565440 | bytes 7045120 | tf_op jit(solution)/shard_map/ind,cdf->cinf/dot_general | solution.py:51
  103.3 4.9 %fusion.80 = (f32[4,512]{1,0:T(4,128)S(1)}, f32[4,512,1024]{2,1,0:T(8,128)}) fusion(f32[1024]{0:T(1024)S(1)} %bitcast.179, bf16[1024,4,80]{0,2,1:T(8,128)(2,1)S(1)} %bitcast.170, bf16[1,1024,4,80]{1,3,2,0:T(8,128)(2,1)S(1)} %bitcast.168), kind=kOutput, calls=%fused_computation.120 | convolution fusion | flops 343933952 | bytes 9383936 | tf_op jit(solution)/shard_map/sub | solution.py:76
  108.2 4.9 %fusion.79 = (f32[4,512]{1,0:T(4,128)S(1)}, f32[4,512,1024]{2,1,0:T(8,128)}) fusion(f32[1024]{0:T(1024)S(1)} %bitcast.180, bf16[1024,4,80]{0,2,1:T(8,128)(2,1)S(1)} %bitcast.171, bf16[1,1024,4,80]{1,3,2,0:T(8,128)(2,1)S(1)} %bitcast.169), kind=kOutput, calls=%fused_computation.119 | convolution fusion | flops 343933952 | bytes 9383936 | tf_op jit(solution)/shard_map/sub | solution.py:76
  113.0 5.1 %fusion.37 = bf16[4,80,512]{2,1,0:T(8,128)(2,1)S(1)} fusion(bf16[1024,4,80]{0,2,1:T(8,128)(2,1)S(1)} %bitcast.166, f32[4,512,1024]{2,1,0:T(8,128)} %get-tuple-element.13, f32[4,512]{1,0:T(4,128)S(1)} %get-tuple-element.12), kind=kOutput, calls=%fused_computation.55 | convolution fusion | flops 339902464 | bytes 9379840 | tf_op jit(solution)/shard_map/ihqk,ikhe->iqhe/dot_general | solution.py:77
  118.1 0.8 copy-done.9
  118.9 1.7 fusion.36
  120.6 4.0 %convolution_multiply_fusion = f32[1024,1280]{1,0:T(8,128)} fusion(bf16[320,1280]{0,1:T(8,128)(2,1)S(1)} %all_gather.20, f32[1024]{0:T(1024)S(1)} %bitcast.165, bf16[1,512,320]{1,2,0:T(8,128)(2,1)S(1)} %bitcast.173, bf16[1,512,320]{1,2,0:T(8,128)(2,1)S(1)} %bitcast.172), kind=kOutput, calls=%fused_computation.24 | convolution fusion | flops 841482240 | bytes 6721536 | tf_op jit(solution)/shard_map/ind,de->ine/dot_general | solution.py:82
  124.6 1.4 constant_dynamic-slice_fusion.2
  126.0 1.3 fusion.35
  127.3 3.1 gather_fusion.1
  130.5 9.7 %gather_fusion = f32[1008,1280]{1,0:T(8,128)} fusion(f32[1024,1280]{1,0:T(8,128)} %fusion.35, s32[1024]{0:T(1024)S(1)} %pad_clamp_fusion.2), kind=kCustom, calls=%fused_computation | custom fusion | bytes 10325952 | tf_op jit(solution)/shard_map/jit(take_along_axis)/gather | solution.py:18
  140.1 5.1 %fusion.21 = bf16[1008,1,1280]{2,0,1:T(8,128)(2,1)S(1)} fusion(f32[1008,1280]{1,0:T(8,128)} %gather_fusion, pred[1008]{0:T(1024)(128)(4,1)S(1)} %compare_and_fusion, f32[16,1280]{1,0:T(8,128)S(1)} %gather_fusion.1, pred[16]{0:T(512)(128)(4,1)S(1)} %compare_and_fusion.1, s32[1008]{0:T(1024)S(1)} %bitcast.175, s32[16]{0:T(128)S(1)} %bitcast.185), kind=kOutput, calls=%fused_computation.33 | convolution fusion | flops 251633408 | bytes 7828480 | tf_op jit(solution)/shard_map/icr,ird->icd/dot_general | solution.py:21
  145.2 27.6 %fusion = bf16[256,1280]{1,0:T(8,128)(2,1)S(1)} fusion(bf16[1008,1,1280]{2,0,1:T(8,128)(2,1)S(1)} %fusion.21), kind=kCustom, calls=%all-reduce-scatter | all-reduce-scatter fusion | flops 1310721 | bytes 3236352
  172.8 4.4 %collective-permute-start = (bf16[12,1280]{1,0:T(8,128)(2,1)S(1)}, bf16[12,1280]{1,0:T(8,128)(2,1)S(1)}, u32[]{:S(2)}, u32[]{:S(2)}) collective-permute-start(bf16[12,1280]{1,0:T(8,128)(2,1)S(1)} %slice.36), channel_id=1, source_target_pairs={{0,1},{1,2},{2,3},{4,5},{5,6},{6,7},{8,9},{9,10},{10,11},{12,13},{... | collective-permute-start | bytes 92168
  178.5 1.1 concatenate.4
  180.9 2.1 copy.14
  183.1 39.2 %all-gather.14.cloned.1.call-done = bf16[1280,1280]{0,1:T(8,128)(2,1)} async-done(((bf16[1280,160]{0,1:T(8,128)(2,1)}), bf16[1280,1280]{0,1:T(8,128)(2,1)}) %all-gather.14.cloned.1.call-update) | async-done | bytes 3276816 | tf_op jit(solution)/shard_map/all_gather | solution.py:125
  222.2 42.2 %all-gather.10.cloned.1.call-done = bf16[1,1008,1280]{2,0,1:T(2,128)(2,1)} async-done(((bf16[1,252,1280]{2,0,1:T(2,128)(2,1)}), bf16[1,1008,1280]{2,0,1:T(2,128)(2,1)}) %all-gather.10.cloned.1.call-update) | async-done | bytes 2580496 | tf_op jit(solution)/shard_map/all_gather | solution.py:113
  264.5 12.8 %fusion.20 = bf16[1,1008,1280]{2,1,0:T(8,128)(2,1)} fusion(bf16[1280,1280]{0,1:T(8,128)(2,1)} %all-gather.14.cloned.1.call-done, bf16[1280,1280]{1,0:T(8,128)(2,1)} %all-gather.12.cloned.1.call-done, bf16[1,1008,1280]{2,0,1:T(2,128)(2,1)} %all-gather.10.cloned.1.call-done, f32[1280]{0:T(1024)S(1)} %copy-done.7), kind=kOutput, calls=%fused_computation.32 | convolution fusion | flops 6620221440 | bytes 11719680 | tf_op jit(solution)/shard_map/imf,fd->imd/dot_general | solution.py:122
  277.3 26.0 %fusion.1 = bf16[256,1280]{1,0:T(8,128)(2,1)S(1)} fusion(bf16[1,1008,1280]{2,1,0:T(8,128)(2,1)} %fusion.20), kind=kCustom, calls=%all-reduce-scatter.1 | all-reduce-scatter fusion | flops 1310721 | bytes 3236352
  303.4 4.4 %collective-permute-start.1 = (bf16[12,1280]{1,0:T(8,128)(2,1)S(1)}, bf16[12,1280]{1,0:T(8,128)(2,1)S(1)}, u32[]{:S(2)}, u32[]{:S(2)}) collective-permute-start(bf16[12,1280]{1,0:T(8,128)(2,1)S(1)} %slice.37), channel_id=1, source_target_pairs={{0,1},{1,2},{2,3},{4,5},{5,6},{6,7},{8,9},{9,10},{10,11},{12,13},{... | collective-permute-start | bytes 92168
  307.8 1.1 collective-permute-done.1
  308.9 1.0 concatenate.5
  309.9 1.3 add_convert_fusion.1
  (54 shorter events, 3.9 us)
Async XLA Ops:
  6.5 7.1 %copy-start.8 = (s32[1,16]{1,0:T(1,128)S(1)}, s32[1,16]{1,0:T(1,128)}, u32[]{:S(2)}) copy-start(s32[1,16]{1,0:T(1,128)} %param.21) | copy-start | bytes 196
  6.5 7.2 %copy-start = (f32[1,1024]{1,0:T(1,128)S(1)}, f32[1,1024]{1,0:T(1,128)}, u32[]{:S(2)}) copy-start(f32[1,1024]{1,0:T(1,128)} %param.13) | copy-start | bytes 12292
  6.5 7.2 %copy-start.2 = (bf16[320,160]{0,1:T(8,128)(2,1)S(1)}, bf16[320,160]{0,1:T(8,128)(2,1)}, u32[]{:S(2)}) copy-start(bf16[320,160]{0,1:T(8,128)(2,1)} %param.16) | copy-start | bytes 307204
  6.5 35.5 %copy-start.3 = (s32[1,1008]{1,0:T(1,128)S(1)}, s32[1,1008]{1,0:T(1,128)}, u32[]{:S(2)}) copy-start(s32[1,1008]{1,0:T(1,128)} %param.23) | copy-start | bytes 12100
  6.5 37.8 %all-gather.6.cloned.1.call-start = ((), (), s32[]{:S(2)}) async-start(), calls=%async_computation | async-start | bytes 3276800 | tf_op jit(solution)/shard_map/all_gather | solution.py:48
  7.9 36.3 %copy-start.5 = (s32[1,16]{1,0:T(1,128)S(1)}, s32[1,16]{1,0:T(1,128)}, u32[]{:S(2)}) copy-start(s32[1,16]{1,0:T(1,128)} %param.22) | copy-start | bytes 196
  11.6 86.2 %all-gather.8.cloned.1.call-start = ((), (), s32[]{:S(2)}) async-start(), calls=%async_computation.1 | async-start | bytes 3317760 | tf_op jit(solution)/shard_map/all_gather | solution.py:54
  12.3 170.7 %all-gather.12.cloned.1.call-start = ((), (), s32[]{:S(2)}) async-start(), calls=%async_computation.3 | async-start | bytes 3686400 | tf_op jit(solution)/shard_map/all_gather | solution.py:118
  13.0 209.2 %all-gather.14.cloned.1.call-start = ((), (), s32[]{:S(2)}) async-start(), calls=%async_computation.4 | async-start | bytes 3686400 | tf_op jit(solution)/shard_map/all_gather | solution.py:125
  13.6 250.8 %all-gather.10.cloned.1.call-start = ((), (), s32[]{:S(2)}) async-start(), calls=%async_computation.2 | async-start | bytes 6451200 | tf_op jit(solution)/shard_map/all_gather | solution.py:113
  113.0 5.9 %copy-start.9 = (f32[4,512,1024]{2,1,0:T(8,128)S(1)}, f32[4,512,1024]{2,1,0:T(8,128)}, u32[]{:S(2)}) copy-start(f32[4,512,1024]{2,1,0:T(8,128)} %get-tuple-element.11) | copy-start | bytes 25165828
  120.6 5.4 %copy-start.1 = (bf16[1,256,1280]{2,1,0:T(8,128)(2,1)S(1)}, bf16[1,256,1280]{2,1,0:T(8,128)(2,1)}, u32[]{:S(2)}) copy-start(bf16[1,256,1280]{2,1,0:T(8,128)(2,1)} %param.12) | copy-start | bytes 1966084
  145.2 32.0 %copy-start.6 = (u32[32]{0:T(128)S(1)}, u32[32]{0:T(128)}, u32[]{:S(2)}) copy-start(u32[32]{0:T(128)} %constant.99) | copy-start | bytes 388
  145.2 35.3 %copy-start.4 = (f32[1280]{0:T(1024)S(1)}, f32[1280]{0:T(1024)}, u32[]{:S(2)}) copy-start(f32[1280]{0:T(1024)} %param.17) | copy-start | bytes 15364
  172.8 5.7 %collective-permute-start = (bf16[12,1280]{1,0:T(8,128)(2,1)S(1)}, bf16[12,1280]{1,0:T(8,128)(2,1)S(1)}, u32[]{:S(2)}, u32[]{:S(2)}) collective-permute-start(bf16[12,1280]{1,0:T(8,128)(2,1)S(1)} %slice.36), channel_id=1, source_target_pairs={{0,1},{1,2},{2,3},{4,5},{5,6},{6,7},{8,9},{9,10},{10,11},{12,13},{... | collective-permute-start | bytes 92168
  179.6 84.9 %copy-start.7 = (f32[1280]{0:T(1024)S(1)}, f32[1280]{0:T(1024)}, u32[]{:S(2)}) copy-start(f32[1280]{0:T(1024)} %param.19) | copy-start | bytes 15364
  303.4 5.5 %collective-permute-start.1 = (bf16[12,1280]{1,0:T(8,128)(2,1)S(1)}, bf16[12,1280]{1,0:T(8,128)(2,1)S(1)}, u32[]{:S(2)}, u32[]{:S(2)}) collective-permute-start(bf16[12,1280]{1,0:T(8,128)(2,1)S(1)} %slice.37), channel_id=1, source_target_pairs={{0,1},{1,2},{2,3},{4,5},{5,6},{6,7},{8,9},{9,10},{10,11},{12,13},{... | collective-permute-start | bytes 92168
Sparse Core Ops, SparseCore 0:
  11.7 27.9 all-gather.5
  41.9 55.8 all-gather.7
  100.0 59.9 all-gather.11
  162.0 60.1 all-gather.13
  223.6 40.7 all-gather.9
where the time goes:
time: 318 us
  waiting for transfers between devices  138 us (43%)
  blocking collectives  81.9 us (26%)
  matrix products  44 us (14%)
  local copies, waits for them, and re-layouts  22 us (7%)
  between operations  14.1 us (4%)
  starting transfers between devices  8.96 us (3%)
  other arithmetic  8.93 us (3%)
    unnamed x2, blocking collectives  53.6 us
    all_gather x1, waiting for transfers between devices, shards(): lax.all_gather(qkv_weight, 'dp', axis=1, tiled=True)  53.4 us
    all_gather x1, waiting for transfers between devices, shards(): gathered = lax.all_gather(normed_two, 'mp', axis=1, tiled=True)  42.2 us
    all_gather x1, waiting for transfers between devices, shards(): lax.all_gather(fc2_weight, 'dp', axis=1, tiled=True)  39.2 us
    all_gather x1, blocking collectives, shards(): lax.all_gather(proj_weight, 'dp', axis=1, tiled=True)  28.3 us
    dot_general x1, matrix products, shards(): jnp.einsum('imf,fd->imd', hidden, lax.all_gather(fc2_weight, 'dp', axis=1...  12.8 us
    gather x2, local copies, waits for them, and re-layouts, merge_rows(): kept_rows = jnp.take_along_axis(total, order_rows[:, :, None], axis=1)  11 us
    sub x2, matrix products, shards(): weights = jax.nn.softmax(scores, axis=-1).astype(jnp.bfloat16)  9.7 us
  transfers between devices with their start and end apart: 7, of which 4 were waited for; matrix products, arithmetic and copies ran while one was open for 26% of the time, Pallas kernels for 0%

commit v1 on v0

--- a/solution.py
+++ b/solution.py
@@ -110,7 +110,12 @@
     merged_size = merge_rows(sizes[:, :, None], own_order, pair_source, pair_target)
     merged = numerator / merged_size
     normed_two = layer_norm(merged, ln2_gain).astype(jnp.bfloat16)
-    gathered = lax.all_gather(normed_two, "mp", axis=1, tiled=True)
+    ring = [normed_two]
+    for hop in range(3):
+        ring.append(lax.ppermute(ring[-1], "mp", [(dev, (dev + 1) % 4) for dev in range(4)]))
+    gathered = jnp.roll(
+        jnp.concatenate(ring[::-1], axis=1), (lax.axis_index("mp") + 1) * ring[0].shape[1], axis=1
+    )
     columns = gathered
     hidden_sum = jnp.einsum(
         "imd,df->imf",

time: 318 us -> 288 us (0.906)
  waiting for transfers between devices: 138 us -> 79 us
  local copies, waits for them, and re-layouts: 22 us -> 42.8 us
  starting transfers between devices: 8.96 us -> 16 us
    all_gather x1 -> x0, waiting for transfers between devices: 42.2 us -> none  [shards(): gathered = lax.all_gather(normed_two, 'mp', axis=1, tiled=True)]
    all_gather x1, waiting for transfers between devices: 39.2 us -> 0.01 us  [shards(): lax.all_gather(fc2_weight, 'dp', axis=1, tiled=True)]
    concatenate x0 -> x1, local copies, waits for them, and re-layouts: none -> 22.8 us  [shards(): jnp.roll(jnp.concatenate(ring[::-1], axis=1), (lax.axis_index('mp') + 1)...]
    ppermute x0 -> x3, waiting for transfers between devices: none -> 22.6 us  [shards(): lax.ppermute(ring[-1], 'mp', [(dev, (dev + 1) % 4) for dev in range(4)])]
    ppermute x0 -> x3, starting transfers between devices: none -> 7.1 us  [shards(): lax.ppermute(ring[-1], 'mp', [(dev, (dev + 1) % 4) for dev in range(4)])]
  transfers between devices with their start and end apart: 7 -> 9, of which waited for: 4 -> 5; matrix products, arithmetic and copies ran while one was open for 26% -> 36% of each run, Pallas kernels for 0% -> 0%
where the time goes in v1:
time: 288 us; the launch traced here: 287 us
  blocking collectives  82.6 us (29%)
  waiting for transfers between devices  79 us (27%)
  matrix products  43.6 us (15%)
  local copies, waits for them, and re-layouts  42.8 us (15%)
  starting transfers between devices  16 us (6%)
  between operations  14.1 us (5%)
  other arithmetic  8.93 us (3%)
    unnamed x2, blocking collectives  54.3 us
    all_gather x1, waiting for transfers between devices, shards(): lax.all_gather(qkv_weight, 'dp', axis=1, tiled=True)  53.4 us
    all_gather x1, blocking collectives, shards(): lax.all_gather(proj_weight, 'dp', axis=1, tiled=True)  28.3 us
    concatenate x1, local copies, waits for them, and re-layouts, shards(): jnp.roll(jnp.concatenate(ring[::-1], axis=1), (lax.axis_index('mp') + 1)...  22.8 us
    ppermute x3, waiting for transfers between devices, shards(): lax.ppermute(ring[-1], 'mp', [(dev, (dev + 1) % 4) for dev in range(4)])  22.6 us
    dot_general x1, matrix products, shards(): jnp.einsum('imf,fd->imd', hidden, lax.all_gather(fc2_weight, 'dp', axis=1...  12.5 us
    gather x2, local copies, waits for them, and re-layouts, merge_rows(): kept_rows = jnp.take_along_axis(total, order_rows[:, :, None], axis=1)  11 us
    sub x2, matrix products, shards(): weights = jax.nn.softmax(scores, axis=-1).astype(jnp.bfloat16)  9.7 us
  transfers between devices with their start and end apart: 9, of which 5 were waited for; matrix products, arithmetic and copies ran while one was open for 36% of the time, Pallas kernels for 0%

profile of v1, /device:TPU:1, one launch (start us, length us, event | category | flops | bytes accessed | tf_op | source)
XLA Modules:
  0.0 287.0 jit_solution(2579341762247655634)
XLA Ops:
  6.6 1.3 convert_reduce_fusion
  7.9 1.4 fusion.30
  9.3 2.2 fusion.32
  13.7 28.3 %all_gather.17 = bf16[320,1280]{0,1:T(8,128)(2,1)S(1)} all-gather(bf16[320,160]{0,1:T(8,128)(2,1)S(1)} %copy-done.2), channel_id=1, replica_groups=mesh['dp'=8,'mp'=4] {'dp'}, dimensions={1}, use_global_device_ids=true | all-gather | bytes 921600 | tf_op jit(solution)/shard_map/all_gather | solution.py:85
  42.8 1.4 gather_fusion.2
  44.3 53.4 %all-gather.7.cloned.1.call-done = bf16[3,1280,320]{2,1,0:T(8,128)(2,1)} async-done(((bf16[3,160,320]{2,1,0:T(8,128)(2,1)}), bf16[3,1280,320]{2,1,0:T(8,128)(2,1)}) %all-gather.7.cloned.1.call-update) | async-done | bytes 2457616 | tf_op jit(solution)/shard_map/all_gather | solution.py:54
  97.8 5.4 %convert_bitcast_fusion = bf16[3,1,1024,320]{2,3,0,1:T(8,128)(2,1)S(1)} fusion(bf16[3,1280,320]{2,1,0:T(8,128)(2,1)} %all-gather.7.cloned.1.call-done, bf16[1,1024,1280]{2,1,0:T(8,128)(2,1)} %all-gather.5.cloned.1.call-done), kind=kOutput, calls=%fused_computation.38 | convolution fusion | flops 2517565440 | bytes 7045120 | tf_op jit(solution)/shard_map/ind,cdf->cinf/dot_general | solution.py:51
  103.3 4.9 %fusion.82 = (f32[4,512]{1,0:T(4,128)S(1)}, f32[4,512,1024]{2,1,0:T(8,128)}) fusion(f32[1024]{0:T(1024)S(1)} %bitcast.179, bf16[1024,4,80]{0,2,1:T(8,128)(2,1)S(1)} %bitcast.170, bf16[1,1024,4,80]{1,3,2,0:T(8,128)(2,1)S(1)} %bitcast.168), kind=kOutput, calls=%fused_computation.121 | convolution fusion | flops 343933952 | bytes 9383936 | tf_op jit(solution)/shard_map/sub | solution.py:76
  108.2 4.9 %fusion.81 = (f32[4,512]{1,0:T(4,128)S(1)}, f32[4,512,1024]{2,1,0:T(8,128)}) fusion(f32[1024]{0:T(1024)S(1)} %bitcast.180, bf16[1024,4,80]{0,2,1:T(8,128)(2,1)S(1)} %bitcast.171, bf16[1,1024,4,80]{1,3,2,0:T(8,128)(2,1)S(1)} %bitcast.169), kind=kOutput, calls=%fused_computation.120 | convolution fusion | flops 343933952 | bytes 9383936 | tf_op jit(solution)/shard_map/sub | solution.py:76
  113.0 5.1 %fusion.37 = bf16[4,80,512]{2,1,0:T(8,128)(2,1)S(1)} fusion(bf16[1024,4,80]{0,2,1:T(8,128)(2,1)S(1)} %bitcast.166, f32[4,512,1024]{2,1,0:T(8,128)} %get-tuple-element.13, f32[4,512]{1,0:T(4,128)S(1)} %get-tuple-element.12), kind=kOutput, calls=%fused_computation.55 | convolution fusion | flops 339902464 | bytes 9379840 | tf_op jit(solution)/shard_map/ihqk,ikhe->iqhe/dot_general | solution.py:77
  118.9 1.7 fusion.36
  120.6 4.0 %convolution_multiply_fusion = f32[1024,1280]{1,0:T(8,128)} fusion(bf16[320,1280]{0,1:T(8,128)(2,1)S(1)} %all_gather.17, f32[1024]{0:T(1024)S(1)} %bitcast.165, bf16[1,512,320]{1,2,0:T(8,128)(2,1)S(1)} %bitcast.173, bf16[1,512,320]{1,2,0:T(8,128)(2,1)S(1)} %bitcast.172), kind=kOutput, calls=%fused_computation.24 | convolution fusion | flops 841482240 | bytes 6721536 | tf_op jit(solution)/shard_map/ind,de->ine/dot_general | solution.py:82
  124.6 1.4 constant_dynamic-slice_fusion.2
  126.0 1.3 fusion.35
  127.3 3.1 %gather_fusion.1 = f32[16,1280]{1,0:T(8,128)S(1)} fusion(f32[1024,1280]{1,0:T(8,128)} %fusion.35, s32[1024]{0:T(1024)S(1)} %pad_clamp_fusion.1), kind=kCustom, calls=%fused_computation.1 | custom fusion | bytes 163904 | tf_op jit(solution)/shard_map/jit(take_along_axis)/gather | solution.py:19
  130.5 9.7 %gather_fusion = f32[1008,1280]{1,0:T(8,128)} fusion(f32[1024,1280]{1,0:T(8,128)} %fusion.35, s32[1024]{0:T(1024)S(1)} %pad_clamp_fusion.2), kind=kCustom, calls=%fused_computation | custom fusion | bytes 10325952 | tf_op jit(solution)/shard_map/jit(take_along_axis)/gather | solution.py:18
  140.1 5.1 %fusion.21 = bf16[1008,1,1280]{2,0,1:T(8,128)(2,1)S(1)} fusion(f32[1008,1280]{1,0:T(8,128)} %gather_fusion, pred[1008]{0:T(1024)(128)(4,1)S(1)} %compare_and_fusion, f32[16,1280]{1,0:T(8,128)S(1)} %gather_fusion.1, pred[16]{0:T(512)(128)(4,1)S(1)} %compare_and_fusion.1, s32[1008]{0:T(1024)S(1)} %bitcast.175, s32[16]{0:T(128)S(1)} %bitcast.185), kind=kOutput, calls=%fused_computation.33 | convolution fusion | flops 251633408 | bytes 7828480 | tf_op jit(solution)/shard_map/icr,ird->icd/dot_general | solution.py:21
  145.2 27.6 %fusion = bf16[256,1280]{1,0:T(8,128)(2,1)S(1)} fusion(bf16[1008,1,1280]{2,0,1:T(8,128)(2,1)S(1)} %fusion.21), kind=kCustom, calls=%all-reduce-scatter | all-reduce-scatter fusion | flops 1310721 | bytes 3236352
  172.8 4.4 %collective-permute-start.3 = (bf16[12,1280]{1,0:T(8,128)(2,1)S(1)}, bf16[12,1280]{1,0:T(8,128)(2,1)S(1)}, u32[]{:S(2)}, u32[]{:S(2)}) collective-permute-start(bf16[12,1280]{1,0:T(8,128)(2,1)S(1)} %slice.36), channel_id=1, source_target_pairs={{0,1},{1,2},{2,3},{4,5},{5,6},{6,7},{8,9},{9,10},{10,11},{12,13},{... | collective-permute-start | bytes 92168
  178.5 1.1 concatenate.11
  180.9 2.1 collective-permute-start
  183.0 7.5 %collective-permute-done = bf16[1,252,1280]{2,1,0:T(8,128)(2,1)S(1)} collective-permute-done((bf16[1,252,1280]{2,1,0:T(8,128)(2,1)S(1)}, bf16[1,252,1280]{2,1,0:T(8,128)(2,1)S(1)}, u32[]{:S(2)}, u32[]{:S(2)}) %collective-permute-start) | collective-permute-done | bytes 645152 | tf_op jit(solution)/shard_map/ppermute | solution.py:115
  190.6 2.5 collective-permute-start.1
  193.1 7.5 %collective-permute-done.1 = bf16[1,252,1280]{2,1,0:T(8,128)(2,1)S(1)} collective-permute-done((bf16[1,252,1280]{2,1,0:T(8,128)(2,1)S(1)}, bf16[1,252,1280]{2,1,0:T(8,128)(2,1)S(1)}, u32[]{:S(2)}, u32[]{:S(2)}) %collective-permute-start.1) | collective-permute-done | bytes 645152 | tf_op jit(solution)/shard_map/ppermute | solution.py:115
  200.6 2.5 collective-permute-start.2
  203.1 7.5 %collective-permute-done.2 = bf16[1,252,1280]{2,1,0:T(8,128)(2,1)S(1)} collective-permute-done((bf16[1,252,1280]{2,1,0:T(8,128)(2,1)S(1)}, bf16[1,252,1280]{2,1,0:T(8,128)(2,1)S(1)}, u32[]{:S(2)}, u32[]{:S(2)}) %collective-permute-start.2) | collective-permute-done | bytes 645152 | tf_op jit(solution)/shard_map/ppermute | solution.py:115
  210.6 22.8 %concatenate.10 = bf16[1,2016,1280]{2,1,0:T(8,128)(2,1)} concatenate(bf16[1,252,1280]{2,1,0:T(8,128)(2,1)S(1)} %collective-permute-done.2, bf16[1,252,1280]{2,1,0:T(8,128)(2,1)S(1)} %collective-permute-done.1, bf16[1,252,1280]{2,1,0:T(8,128)(2,1)S(1)} %collective-permute-done, bf16[1,252,1280]{2,1,0:T(8,128)(2,1)S(1)} %multiply_convert_fusion, ...), dimensions={1} | concatenate | bytes 10321920 | tf_op jit(solution)/shard_map/jit(_roll_dynamic)/concatenate | solution.py:116
  233.5 12.5 %fusion.20 = bf16[1,1008,1280]{2,1,0:T(8,128)(2,1)} fusion(bf16[1280,1280]{0,1:T(8,128)(2,1)} %all-gather.11.cloned.1.call-done, bf16[1280,1280]{1,0:T(8,128)(2,1)} %all-gather.9.cloned.1.call-done, f32[1280]{0:T(1024)S(1)} %copy-done.7, bf16[1,2016,1280]{2,1,0:T(8,128)(2,1)} %concatenate.10, s32[]{:T(128)S(6)} %select_n.178), kind=kOutput, calls=%fused_computation.32 | convolution fusion | flops 6620221440 | bytes 11719684 | tf_op jit(solution)/shard_map/imf,fd->imd/dot_general | solution.py:127
  246.0 26.7 %fusion.1 = bf16[256,1280]{1,0:T(8,128)(2,1)S(1)} fusion(bf16[1,1008,1280]{2,1,0:T(8,128)(2,1)} %fusion.20), kind=kCustom, calls=%all-reduce-scatter.1 | all-reduce-scatter fusion | flops 1310721 | bytes 3236352
  272.7 4.4 %collective-permute-start.4 = (bf16[12,1280]{1,0:T(8,128)(2,1)S(1)}, bf16[12,1280]{1,0:T(8,128)(2,1)S(1)}, u32[]{:S(2)}, u32[]{:S(2)}) collective-permute-start(bf16[12,1280]{1,0:T(8,128)(2,1)S(1)} %slice.37), channel_id=1, source_target_pairs={{0,1},{1,2},{2,3},{4,5},{5,6},{6,7},{8,9},{9,10},{10,11},{12,13},{... | collective-permute-start | bytes 92168
  277.1 1.1 collective-permute-done.4
  279.3 1.3 add_convert_fusion.1
  (57 shorter events, 7.0 us)
Async XLA Ops:
  6.5 7.1 %copy-start.8 = (s32[1,16]{1,0:T(1,128)S(1)}, s32[1,16]{1,0:T(1,128)}, u32[]{:S(2)}) copy-start(s32[1,16]{1,0:T(1,128)} %param.21) | copy-start | bytes 196
  6.5 7.1 %copy-start = (f32[1,1024]{1,0:T(1,128)S(1)}, f32[1,1024]{1,0:T(1,128)}, u32[]{:S(2)}) copy-start(f32[1,1024]{1,0:T(1,128)} %param.13) | copy-start | bytes 12292
  6.5 7.2 %copy-start.2 = (bf16[320,160]{0,1:T(8,128)(2,1)S(1)}, bf16[320,160]{0,1:T(8,128)(2,1)}, u32[]{:S(2)}) copy-start(bf16[320,160]{0,1:T(8,128)(2,1)} %param.16) | copy-start | bytes 307204
  6.5 35.4 %copy-start.3 = (s32[1,1008]{1,0:T(1,128)S(1)}, s32[1,1008]{1,0:T(1,128)}, u32[]{:S(2)}) copy-start(s32[1,1008]{1,0:T(1,128)} %param.23) | copy-start | bytes 12100
  6.5 37.8 %all-gather.5.cloned.1.call-start = ((), (), s32[]{:S(2)}) async-start(), calls=%async_computation | async-start | bytes 3276800 | tf_op jit(solution)/shard_map/all_gather | solution.py:48
  7.9 36.2 %copy-start.5 = (s32[1,16]{1,0:T(1,128)S(1)}, s32[1,16]{1,0:T(1,128)}, u32[]{:S(2)}) copy-start(s32[1,16]{1,0:T(1,128)} %param.22) | copy-start | bytes 196
  11.6 86.2 %all-gather.7.cloned.1.call-start = ((), (), s32[]{:S(2)}) async-start(), calls=%async_computation.1 | async-start | bytes 3317760 | tf_op jit(solution)/shard_map/all_gather | solution.py:54
  12.3 221.1 %all-gather.11.cloned.1.call-start = ((), (), s32[]{:S(2)}) async-start(), calls=%async_computation.3 | async-start | bytes 3686400 | tf_op jit(solution)/shard_map/all_gather | solution.py:130
  13.0 220.4 %all-gather.9.cloned.1.call-start = ((), (), s32[]{:S(2)}) async-start(), calls=%async_computation.2 | async-start | bytes 3686400 | tf_op jit(solution)/shard_map/all_gather | solution.py:123
  113.0 5.9 %copy-start.9 = (f32[4,512,1024]{2,1,0:T(8,128)S(1)}, f32[4,512,1024]{2,1,0:T(8,128)}, u32[]{:S(2)}) copy-start(f32[4,512,1024]{2,1,0:T(8,128)} %get-tuple-element.11) | copy-start | bytes 25165828
  120.6 5.4 %copy-start.1 = (bf16[1,256,1280]{2,1,0:T(8,128)(2,1)S(1)}, bf16[1,256,1280]{2,1,0:T(8,128)(2,1)}, u32[]{:S(2)}) copy-start(bf16[1,256,1280]{2,1,0:T(8,128)(2,1)} %param.12) | copy-start | bytes 1966084
  145.2 32.0 %copy-start.6 = (u32[32]{0:T(128)S(1)}, u32[32]{0:T(128)}, u32[]{:S(2)}) copy-start(u32[32]{0:T(128)} %constant.118) | copy-start | bytes 388
  145.2 35.3 %copy-start.4 = (f32[1280]{0:T(1024)S(1)}, f32[1280]{0:T(1024)}, u32[]{:S(2)}) copy-start(f32[1280]{0:T(1024)} %param.17) | copy-start | bytes 15364
  172.8 5.7 %collective-permute-start.3 = (bf16[12,1280]{1,0:T(8,128)(2,1)S(1)}, bf16[12,1280]{1,0:T(8,128)(2,1)S(1)}, u32[]{:S(2)}, u32[]{:S(2)}) collective-permute-start(bf16[12,1280]{1,0:T(8,128)(2,1)S(1)} %slice.36), channel_id=1, source_target_pairs={{0,1},{1,2},{2,3},{4,5},{5,6},{6,7},{8,9},{9,10},{10,11},{12,13},{... | collective-permute-start | bytes 92168
  180.9 9.7 %collective-permute-start = (bf16[1,252,1280]{2,1,0:T(8,128)(2,1)S(1)}, bf16[1,252,1280]{2,1,0:T(8,128)(2,1)S(1)}, u32[]{:S(2)}, u32[]{:S(2)}) collective-permute-start(bf16[1,252,1280]{2,1,0:T(8,128)(2,1)S(1)} %multiply_convert_fusion), channel_id=1, source_target_pairs={{0,1},{1,2},{2,3},{3,0},{4,5},{5,6},{6,7},{7,4},{8,9},{9,10},{10,1... | collective-permute-start | bytes 1935368 | tf_op jit(solution)/shard_map/ppermute | solution.py:115
  190.6 10.0 %collective-permute-start.1 = (bf16[1,252,1280]{2,1,0:T(8,128)(2,1)S(1)}, bf16[1,252,1280]{2,1,0:T(8,128)(2,1)S(1)}, u32[]{:S(2)}, u32[]{:S(2)}) collective-permute-start(bf16[1,252,1280]{2,1,0:T(8,128)(2,1)S(1)} %collective-permute-done), channel_id=1, source_target_pairs={{0,1},{1,2},{2,3},{3,0},{4,5},{5,6},{6,7},{7,4},{8,9},{9,10},{10,1... | collective-permute-start | bytes 1935368 | tf_op jit(solution)/shard_map/ppermute | solution.py:115
  200.6 10.0 %collective-permute-start.2 = (bf16[1,252,1280]{2,1,0:T(8,128)(2,1)S(1)}, bf16[1,252,1280]{2,1,0:T(8,128)(2,1)S(1)}, u32[]{:S(2)}, u32[]{:S(2)}) collective-permute-start(bf16[1,252,1280]{2,1,0:T(8,128)(2,1)S(1)} %collective-permute-done.1), channel_id=1, source_target_pairs={{0,1},{1,2},{2,3},{3,0},{4,5},{5,6},{6,7},{7,4},{8,9},{9,10},{10,1... | collective-permute-start | bytes 1935368 | tf_op jit(solution)/shard_map/ppermute | solution.py:115
  203.1 30.4 %copy-start.7 = (f32[1280]{0:T(1024)S(1)}, f32[1280]{0:T(1024)}, u32[]{:S(2)}) copy-start(f32[1280]{0:T(1024)} %param.19) | copy-start | bytes 15364
  272.7 5.5 %collective-permute-start.4 = (bf16[12,1280]{1,0:T(8,128)(2,1)S(1)}, bf16[12,1280]{1,0:T(8,128)(2,1)S(1)}, u32[]{:S(2)}, u32[]{:S(2)}) collective-permute-start(bf16[12,1280]{1,0:T(8,128)(2,1)S(1)} %slice.37), channel_id=1, source_target_pairs={{0,1},{1,2},{2,3},{4,5},{5,6},{6,7},{8,9},{9,10},{10,11},{12,13},{... | collective-permute-start | bytes 92168
Sparse Core Ops, SparseCore 0:
  11.7 27.9 all-gather.4
  41.9 55.8 all-gather.6
  100.0 59.9 all-gather.10
  162.0 60.1 all-gather.8
